TPU v7x, 32 devices: a whole 2x2x4 slice. The times are simulated.
32 devices in a mesh: vocab: 8 (over z, y), batch: 4 (over x, core).
Axes of the slice: x: 2, y: 2, z: 4, core: 2. Of those that a mesh axis runs over, the one named last changes fastest.
Arguments:
- latent_state_rows: bfloat16 [64, 8192], P('batch', 'vocab'), may hold values from -90 to 90
- closing_rescale_coeffs: bfloat16 [8192], replicated, may hold values from 0.5 to 1.5
- output_projection_matrix: bfloat16 [8192, 131072], P(None, ('vocab', 'batch')), may hold values from -3.7565048 to 3.7565048
- config_heat_values: float32 [16], replicated, may hold values from 0.7 to 1.4
- sequence_config_choice: int32 [64], replicated, may hold values from 0 to 15
- ranked_choice_ids: int32 [64, 128], replicated, may hold values from 0 to 131071
- keep_count: int32 [64], replicated, may hold values from 2 to 128
Outputs:
- log_norm: float32 [64], P('batch')
- kept_mass: float32 [64], P('batch')
- renormed: float32 [64, 128], P('batch')
All inputs are finite; a program needn't handle non-finite values.
Results may differ from a plain program's by a relative error of at most 0.0048.
Values may be sent and summed in bfloat16 or wider, within the bound.
No kernel may reach another device: no remote copies, remote signals or barrier semaphores. Data moves between devices by JAX's collectives and lax.ppermute only.
A program may use at most 128 MiB of HBM per device.

v0:
```python
import jax
import jax.numpy as jnp
from jax import lax
from jax.sharding import PartitionSpec as P

epsilon = 1e-06


def normalize(values, gain_part, mean_square):
    factor = lax.rsqrt(mean_square + epsilon)
    return (values * factor[:, None] * gain_part[None, :]).astype(jnp.bfloat16)


def rows_normed(raw_rows, gain_full):
    values = raw_rows.astype(jnp.float32)
    return normalize(values, gain_full, jnp.mean(values * values, axis=1))


def local(
    latent_state_rows,
    closing_rescale_coeffs,
    output_projection_matrix,
    config_heat_values,
    sequence_config_choice,
    ranked_choice_ids,
    keep_count,
):
    group_rows = latent_state_rows.shape[0]
    col_count = output_projection_matrix.shape[1]
    batch_count = lax.axis_size("batch")
    vocab_pos = lax.axis_index("vocab")
    batch_pos = lax.axis_index("batch")
    gain_full = closing_rescale_coeffs.astype(jnp.float32)
    wide_rows = lax.all_gather(latent_state_rows, "vocab", axis=1, tiled=True)
    unnormalized_scores = jnp.dot(
        rows_normed(lax.all_gather(wide_rows, "batch", axis=0, tiled=True), gain_full),
        output_projection_matrix,
        preferred_element_type=jnp.float32,
    )
    config_membership = (
        sequence_config_choice[:, None]
        == jnp.arange(config_heat_values.shape[0], dtype=jnp.int32)[None, :]
    ).astype(jnp.float32)
    sequence_heat_values = jnp.sum(config_membership * config_heat_values[None, :], axis=1)
    divided_scores = unnormalized_scores / sequence_heat_values[:, None]
    offset = (vocab_pos * batch_count + batch_pos) * col_count
    local_ids = ranked_choice_ids - offset
    owned = (local_ids >= 0) & (local_ids < col_count)
    picked = jnp.take_along_axis(divided_scores, jnp.clip(local_ids, 0, col_count - 1), axis=1)
    cand_local = jnp.where(owned, picked, jnp.float32(0.0))
    local_top = jnp.max(divided_scores, axis=1)
    first_slot = batch_pos * group_rows
    row_top = lax.pmax(local_top, ("vocab", "batch"))
    row_total = lax.psum(
        jnp.sum(jnp.exp(divided_scores - row_top[:, None]), axis=1), ("vocab", "batch")
    )
    cand_logit = lax.psum(cand_local, ("vocab", "batch"))
    own_top = lax.dynamic_slice_in_dim(row_top, first_slot, group_rows)
    own_total = lax.dynamic_slice_in_dim(row_total, first_slot, group_rows)
    own_cand = lax.dynamic_slice_in_dim(cand_logit, first_slot, group_rows, 0)
    own_cutoff = lax.dynamic_slice_in_dim(keep_count, first_slot, group_rows)
    log_norm = own_top + jnp.log(own_total)
    kept_mask = jnp.arange(own_cand.shape[1], dtype=jnp.int32)[None, :] < own_cutoff[:, None]
    kept_top = jnp.max(jnp.where(kept_mask, own_cand, jnp.float32(-3e38)), axis=1)
    shifted = jnp.where(kept_mask, own_cand - kept_top[:, None], jnp.float32(0.0))
    kept_exp = jnp.where(kept_mask, jnp.exp(shifted), jnp.float32(0.0))
    kept_sum = jnp.sum(kept_exp, axis=1)
    kept_mass = kept_top + jnp.log(kept_sum) - log_norm
    return (log_norm, kept_mass, kept_exp / kept_sum[:, None])


def solution(mesh):
    placed = (P("batch", "vocab"), P(), P(None, ("vocab", "batch")), P(), P(), P(), P())
    return jax.shard_map(
        local,
        mesh=mesh,
        in_specs=placed,
        out_specs=(P("batch"), P("batch"), P("batch", None)),
        check_vma=False,
    )
```

profile of v0, /device:TPU:0, one launch (start us, length us, event | category | flops | bytes accessed | tf_op | source)
XLA Modules:
  0.0 239.7 jit_solution(4070689631893379016)
XLA Ops:
  7.2 0.0 all-gather.2.cloned.1.call-start
  7.2 34.8 %all_gather.6 = bf16[16,8192]{1,0:T(8,128)(2,1)} all-gather(bf16[16,1024]{1,0:T(8,128)(2,1)} %param.7), channel_id=1, replica_groups=mesh['vocab'=8,'batch'=4] {'vocab'}, dimensions={1}, use_global_device_ids=true | all-gather | bytes 294912 | tf_op jit(solution)/shard_map/all_gather | solution.py:34
  42.0 0.0 all-gather.2.cloned.1.call-update
  42.0 0.7 convert_element_type.11
  42.7 0.7 dynamic_slice.14
  43.5 0.8 select_reduce_fusion.1
  44.2 0.8 fusion.7
  45.0 14.8 %all-gather.2.cloned.1.call-done = bf16[64,8192]{1,0:T(8,128)(2,1)} async-done(((bf16[16,8192]{1,0:T(8,128)(2,1)}), bf16[64,8192]{1,0:T(8,128)(2,1)}) %all-gather.2.cloned.1.call-update) | async-done | bytes 1048592 | tf_op jit(solution)/shard_map/all_gather | solution.py:36
  59.8 1.5 fusion
  61.3 23.9 %fusion.10 = (f32[64]{0:T(128)S(1)}, f32[64,4096]{1,0:T(8,128)S(1)}) fusion(f32[64]{0:T(128)S(1)} %select_reduce_fusion.1, bf16[8192,4096]{1,0:T(8,128)(2,1)} %param.9, bf16[64,8192]{1,0:T(8,128)(2,1)} %all-gather.2.cloned.1.call-done, f32[8192]{0:T(1024)S(1)} %convert_element_type.11, f32[64]{0:T(128)S(1)} %add_rsqrt_fusion), kind=kOutput, calls=%fused_computation.25 | convolution fusion | flops 4297588736 | bytes 69239552 | tf_op jit(solution)/shard_map/dot_general | solution.py:35
  85.2 0.0 copy-start
  85.2 65.0 %gather_fusion = f32[8192]{0:T(1024)S(1)} fusion(f32[64,4096]{1,0:T(8,128)S(1)} %get-tuple-element.8, s32[8192]{0:T(1024)S(1)} %fusion.7), kind=kCustom, calls=%fused_computation | custom fusion | bytes 131072 | tf_op jit(solution)/shard_map/jit(take_along_axis)/gather | solution.py:49
  150.3 0.0 copy-done
  150.3 39.3 %pmax.7 = f32[64]{0:T(128)S(1)} all-reduce(f32[64]{0:T(128)S(1)} %get-tuple-element.7), channel_id=1, replica_groups=mesh['vocab'=8,'batch'=4] {'vocab','batch'}, use_global_device_ids=true, to_apply=%region_3.4 | all-reduce | flops 64 | bytes 512 | tf_op jit(solution)/shard_map/pmax | solution.py:53
  189.6 0.3 exponential_reduce_fusion
  189.9 41.3 %all-reduce = (f32[64]{0:T(128)S(1)}, f32[64,128]{1,0:T(8,128)S(1)}) all-reduce(f32[64]{0:T(128)S(1)} %exponential_reduce_fusion, f32[64,128]{1,0:T(8,128)S(1)} %fusion.6), channel_id=1, replica_groups=mesh['vocab'=8,'batch'=4] {'vocab','batch'}, use_global_device_ids=true, to_apply=%region_5.6 | all-reduce | flops 8256 | bytes 66048 | tf_op jit(solution)/shard_map/psum | solution.py:54
  231.2 0.2 select_reduce_fusion
  231.4 0.2 fusion.9
  231.6 0.7 fusion.8
  232.3 0.6 add_subtract_fusion
  (2 shorter events, 0.0 us)
Async XLA Ops:
  7.2 52.6 %all-gather.2.cloned.1.call-start = ((), (), s32[]{:S(2)}) async-start(), calls=%async_computation | async-start | bytes 1310720 | tf_op jit(solution)/shard_map/all_gather | solution.py:36
  85.2 65.0 %copy-start = (s32[64,128]{1,0:T(8,128)S(1)}, s32[64,128]{1,0:T(8,128)}, u32[]{:S(2)}) copy-start(s32[64,128]{1,0:T(8,128)} %param.12) | copy-start | bytes 98308
Sparse Core Ops, SparseCore 0:
  42.1 17.5 all-gather.1
where the time goes:
time: 240 us
  blocking collectives  115 us (48%)
  local copies, waits for them, and re-layouts  65.7 us (27%)
  matrix products  23.9 us (10%)
  waiting for transfers between devices  14.8 us (6%)
  between operations  14.1 us (6%)
  other arithmetic  5.8 us (2%)
    gather x1, local copies, waits for them, and re-layouts, local(): jnp.take_along_axis(divided_scores, jnp.clip(local_ids, 0, col_count - 1)...  65 us
    psum x1, blocking collectives, local(): lax.psum(jnp.sum(jnp.exp(divided_scores - row_top[:, None]), axis=1), ('v...  41.3 us
    pmax x1, blocking collectives, local(): row_top = lax.pmax(local_top, ('vocab', 'batch'))  39.3 us
    all_gather x1, blocking collectives, local(): wide_rows = lax.all_gather(latent_state_rows, 'vocab', axis=1, tiled=True)  34.8 us
    dot_general x1, matrix products, local(): jnp.dot(rows_normed(lax.all_gather(wide_rows, 'batch', axis=0, tiled=True...  23.9 us
    all_gather x1, waiting for transfers between devices, local(): lax.all_gather(wide_rows, 'batch', axis=0, tiled=True)  14.8 us
  transfers between devices with their start and end apart: 1, of which 1 were waited for; matrix products, arithmetic and copies ran while one was open for 1% of the time, Pallas kernels for 0%

commit v1 on v0

--- a/solution.py
+++ b/solution.py
@@ -51,9 +51,8 @@
     local_top = jnp.max(divided_scores, axis=1)
     first_slot = batch_pos * group_rows
     row_top = lax.pmax(local_top, ("vocab", "batch"))
-    row_total = lax.psum(
-        jnp.sum(jnp.exp(divided_scores - row_top[:, None]), axis=1), ("vocab", "batch")
-    )
+    inner = lax.psum(jnp.sum(jnp.exp(divided_scores - row_top[:, None]), axis=1), "batch")
+    row_total = lax.psum(inner, "vocab")
     cand_logit = lax.psum(cand_local, ("vocab", "batch"))
     own_top = lax.dynamic_slice_in_dim(row_top, first_slot, group_rows)
     own_total = lax.dynamic_slice_in_dim(row_total, first_slot, group_rows)

time: 240 us -> 267 us (1.11)
  blocking collectives: 115 us -> 142 us
    psum x1 -> x3, blocking collectives: 41.3 us -> 66.5 us  [the longest x1 39.4 us: local(): cand_logit = lax.psum(cand_local, ('vocab', 'batch'))]
where the time goes in v1:
time: 267 us
  blocking collectives  142 us (53%)
  local copies, waits for them, and re-layouts  65.7 us (25%)
  matrix products  23.9 us (9%)
  waiting for transfers between devices  14.8 us (6%)
  between operations  14.1 us (5%)
  other arithmetic  5.78 us (2%)
    gather x1, local copies, waits for them, and re-layouts, local(): jnp.take_along_axis(divided_scores, jnp.clip(local_ids, 0, col_count - 1)...  65 us
    pmax x1, blocking collectives, local(): row_top = lax.pmax(local_top, ('vocab', 'batch'))  40.9 us
    psum x1, blocking collectives, local(): cand_logit = lax.psum(cand_local, ('vocab', 'batch'))  39.4 us
    all_gather x1, blocking collectives, local(): wide_rows = lax.all_gather(latent_state_rows, 'vocab', axis=1, tiled=True)  34.8 us
    dot_general x1, matrix products, local(): jnp.dot(rows_normed(lax.all_gather(wide_rows, 'batch', axis=0, tiled=True...  23.9 us
    psum x1, blocking collectives, local(): row_total = lax.psum(inner, 'vocab')  21.3 us
    all_gather x1, waiting for transfers between devices, local(): lax.all_gather(wide_rows, 'batch', axis=0, tiled=True)  14.8 us
    psum x1, blocking collectives, local(): lax.psum(jnp.sum(jnp.exp(divided_scores - row_top[:, None]), axis=1), 'ba...  5.83 us
  transfers between devices with their start and end apart: 1, of which 1 were waited for; matrix products, arithmetic and copies ran while one was open for 1% of the time, Pallas kernels for 0%

profile of v1, /device:TPU:0, one launch (start us, length us, event | category | flops | bytes accessed | tf_op | source)
XLA Modules:
  0.0 266.6 jit_solution(9997333788093067045)
XLA Ops:
  7.2 0.0 all-gather.2.cloned.1.call-start
  7.2 34.8 %all_gather.6 = bf16[16,8192]{1,0:T(8,128)(2,1)} all-gather(bf16[16,1024]{1,0:T(8,128)(2,1)} %param.7), channel_id=1, replica_groups=mesh['vocab'=8,'batch'=4] {'vocab'}, dimensions={1}, use_global_device_ids=true | all-gather | bytes 294912 | tf_op jit(solution)/shard_map/all_gather | solution.py:34
  42.0 0.0 all-gather.2.cloned.1.call-update
  42.0 0.7 convert_element_type.11
  42.7 0.7 dynamic_slice.14
  43.5 0.8 select_reduce_fusion.1
  44.2 0.8 fusion.7
  45.0 14.8 %all-gather.2.cloned.1.call-done = bf16[64,8192]{1,0:T(8,128)(2,1)} async-done(((bf16[16,8192]{1,0:T(8,128)(2,1)}), bf16[64,8192]{1,0:T(8,128)(2,1)}) %all-gather.2.cloned.1.call-update) | async-done | bytes 1048592 | tf_op jit(solution)/shard_map/all_gather | solution.py:36
  59.8 1.5 fusion
  61.3 23.9 %fusion.10 = (f32[64]{0:T(128)S(1)}, f32[64,4096]{1,0:T(8,128)S(1)}) fusion(f32[64]{0:T(128)S(1)} %select_reduce_fusion.1, bf16[8192,4096]{1,0:T(8,128)(2,1)} %param.9, bf16[64,8192]{1,0:T(8,128)(2,1)} %all-gather.2.cloned.1.call-done, f32[8192]{0:T(1024)S(1)} %convert_element_type.11, f32[64]{0:T(128)S(1)} %add_rsqrt_fusion), kind=kOutput, calls=%fused_computation.25 | convolution fusion | flops 4297588736 | bytes 69239552 | tf_op jit(solution)/shard_map/dot_general | solution.py:35
  85.2 0.0 copy-start
  85.2 65.0 %gather_fusion = f32[8192]{0:T(1024)S(1)} fusion(f32[64,4096]{1,0:T(8,128)S(1)} %get-tuple-element.6, s32[8192]{0:T(1024)S(1)} %fusion.7), kind=kCustom, calls=%fused_computation | custom fusion | bytes 131072 | tf_op jit(solution)/shard_map/jit(take_along_axis)/gather | solution.py:49
  150.3 0.0 copy-done
  150.3 39.4 %psum.23 = f32[64,128]{1,0:T(8,128)S(1)} all-reduce(f32[64,128]{1,0:T(8,128)S(1)} %fusion.6), channel_id=1, replica_groups=mesh['vocab'=8,'batch'=4] {'vocab','batch'}, use_global_device_ids=true, to_apply=%region_7.8 | all-reduce | flops 8192 | bytes 65536 | tf_op jit(solution)/shard_map/psum | solution.py:56
  189.8 0.2 select_reduce_fusion
  189.9 0.2 fusion.9
  190.1 40.9 %pmax.7 = f32[64]{0:T(128)S(1)} all-reduce(f32[64]{0:T(128)S(1)} %get-tuple-element.5), channel_id=1, replica_groups=mesh['vocab'=8,'batch'=4] {'vocab','batch'}, use_global_device_ids=true, to_apply=%region_3.4 | all-reduce | flops 64 | bytes 512 | tf_op jit(solution)/shard_map/pmax | solution.py:53
  231.1 0.3 exponential_reduce_fusion
  231.4 5.8 %psum.21 = f32[64]{0:T(128)S(1)} all-reduce(f32[64]{0:T(128)S(1)} %exponential_reduce_fusion), channel_id=1, replica_groups=mesh['vocab'=8,'batch'=4] {'batch'}, use_global_device_ids=true, to_apply=%region_5.6 | all-reduce | flops 64 | bytes 512 | tf_op jit(solution)/shard_map/psum | solution.py:54
  237.2 21.3 %psum.22 = f32[64]{0:T(128)S(1)} all-reduce(f32[64]{0:T(128)S(1)} %psum.21), channel_id=1, replica_groups=mesh['vocab'=8,'batch'=4] {'vocab'}, use_global_device_ids=true, to_apply=%region_6.7 | all-reduce | flops 64 | bytes 512 | tf_op jit(solution)/shard_map/psum | solution.py:55
  258.5 0.7 fusion.8
  259.2 0.6 add_subtract_fusion
  (2 shorter events, 0.0 us)
Async XLA Ops:
  7.2 52.6 %all-gather.2.cloned.1.call-start = ((), (), s32[]{:S(2)}) async-start(), calls=%async_computation | async-start | bytes 1310720 | tf_op jit(solution)/shard_map/all_gather | solution.py:36
  85.2 65.0 %copy-start = (s32[64,128]{1,0:T(8,128)S(1)}, s32[64,128]{1,0:T(8,128)}, u32[]{:S(2)}) copy-start(s32[64,128]{1,0:T(8,128)} %param.12) | copy-start | bytes 98308
Sparse Core Ops, SparseCore 0:
  42.1 17.5 all-gather.1
